TPU v7x, 32 devices: a whole 2x2x4 slice. The times are simulated.
32 devices in a mesh: dp: 4 (over y, x), tp: 8 (over z, core).
Axes of the slice: x: 2, y: 2, z: 4, core: 2. Of those that a mesh axis runs over, the one named last changes fastest.
Arguments:
- proj_in: bfloat16 [1, 4096, 8192], P(None, 'dp', 'tp'), may hold values from -6 to 6
- kv_grad: bfloat16 [1, 4096, 2048], P(None, ('dp', 'tp')), may hold values from -0.1796875 to 0.1796875
- normed: bfloat16 [1, 4096, 8192], P(None, ('dp', 'tp')), may hold values from -6 to 6
- norm_grad: bfloat16 [1, 4096, 8192], P(None, ('dp', 'tp')), may hold values from -0.6 to 0.6
- first_moment: float32 [1, 8192, 2048], P(None, 'tp', 'dp'), may hold values from -0.6 to 0.6
- second_moment: float32 [1, 8192, 2048], P(None, 'tp', 'dp'), may hold values from 0.002 to 0.02
Outputs:
- new_first: float32 [1, 8192, 2048], P(None, 'tp', 'dp')
- new_second: float32 [1, 8192, 2048], P(None, 'tp', 'dp')
- adam_step: float32 [1, 8192, 2048], P(None, 'tp', 'dp')
- gain_grad: float32 [1, 8192], replicated
All inputs are finite; a program needn't handle non-finite values.
Results may differ from a plain program's by a relative error of at most 0.0003.
Values may be sent and summed in bfloat16 or wider, within the bound.
A program may use at most 128 MiB of HBM per device.

v0:
```python
import jax
import jax.numpy as jnp
from jax import lax
from jax.sharding import PartitionSpec as P

beta_one = 0.9
beta_two = 0.95
correct_one = 0.19
correct_two = 0.0975
epsilon = 1e-08


def adam_update(mean_grad, first_old, second_old):
    new_first = beta_one * first_old + (1.0 - beta_one) * mean_grad
    new_second = beta_two * second_old + (1.0 - beta_two) * mean_grad * mean_grad
    update = new_first / correct_one / (jnp.sqrt(new_second / correct_two) + epsilon)
    return (new_first, new_second, update)


def row_adder(inputs, arrived):
    return lax.dot_general(
        inputs, arrived, (((0,), (0,)), ((), ())), preferred_element_type=jnp.float32
    )


def shards(proj_in, kv_grad, normed, norm_grad, first_moment, second_moment):
    replicas = lax.axis_size("dp")
    local_terms = jnp.sum(norm_grad.astype(jnp.float32) * normed.astype(jnp.float32), axis=1)
    gain_grad = lax.psum(local_terms, ("dp", "tp")) / replicas
    inputs = proj_in[0]
    grad_rows = kv_grad[0]
    local_grad = row_adder(inputs, lax.all_gather(grad_rows, "tp", axis=0, tiled=True))
    mean_grad = lax.psum_scatter(local_grad, "dp", scatter_dimension=1, tiled=True) / replicas
    new_first, new_second, update = adam_update(mean_grad, first_moment[0], second_moment[0])
    firsts = [new_first]
    seconds = [new_second]
    updates = [update]
    return (jnp.stack(firsts), jnp.stack(seconds), jnp.stack(updates), gain_grad)


def solution(mesh):
    return jax.shard_map(
        shards,
        mesh=mesh,
        in_specs=(
            P(None, "dp", "tp"),
            P(None, ("dp", "tp"), None),
            P(None, ("dp", "tp"), None),
            P(None, ("dp", "tp"), None),
            P(None, "tp", "dp"),
            P(None, "tp", "dp"),
        ),
        out_specs=(P(None, "tp", "dp"), P(None, "tp", "dp"), P(None, "tp", "dp"), P()),
        check_vma=False,
    )
```

profile of v0, /device:TPU:0, one launch (start us, length us, event | category | flops | bytes accessed | tf_op | source)
XLA Modules:
  0.0 168.0 jit_solution(9199358891031246904)
XLA Ops:
  7.2 0.0 copy-start
  7.2 0.0 all-gather.3.cloned.1.call-start
  7.2 0.7 all-gather.3.cloned.1.call-update
  7.9 0.0 reduce-scatter.2.cloned.1.call-start
  8.0 51.2 %all-gather.3.cloned.1.call-done = bf16[1,1024,2048]{2,1,0:T(8,128)(2,1)} async-done(((bf16[1,128,2048]{2,1,0:T(8,128)(2,1)}), bf16[1,1024,2048]{2,1,0:T(8,128)(2,1)}) %all-gather.3.cloned.1.call-update) | async-done | bytes 4194320 | tf_op jit(solution)/shard_map/all_gather | solution.py:32
  59.2 0.0 copy-done
  59.2 9.0 %fusion = f32[1024,2048]{1,0:T(8,128)} fusion(bf16[1,1024,2048]{2,1,0:T(8,128)(2,1)} %all-gather.3.cloned.1.call-done, bf16[1,1024,1024]{2,1,0:T(8,128)(2,1)S(1)} %copy-done), kind=kOutput, calls=%fused_computation | convolution fusion | flops 4294967296 | bytes 14680064 | tf_op jit(solution)/shard_map/dot_general | solution.py:21
  68.2 0.0 reduce-scatter.2.cloned.1.call-update
  68.2 2.8 %multiply_reduce_fusion = f32[8192]{0:T(1024)S(1)} fusion(bf16[1,128,8192]{2,1,0:T(8,128)(2,1)} %param.8, bf16[1,128,8192]{2,1,0:T(8,128)(2,1)} %param.9), kind=kLoop, calls=%fused_computation.2 | loop fusion | flops 4186112 | bytes 4227072 | tf_op jit(solution)/shard_map/reduce_sum | solution.py:28
  71.0 40.4 %psum.7 = f32[1,8192]{1,0:T(1,128)S(1)} all-reduce(f32[1,8192]{1,0:T(1,128)S(1)} %bitcast.25), channel_id=1, replica_groups=mesh['dp'=4,'tp'=8] {'dp','tp'}, use_global_device_ids=true, to_apply=%region_2.0 | all-reduce | flops 8192 | bytes 65536 | tf_op jit(solution)/shard_map/psum | solution.py:29
  111.4 0.6 broadcast_multiply_fusion
  112.0 42.7 %reduce-scatter.2.cloned.1.call-done = f32[1024,512]{1,0:T(8,128)} async-done(((f32[1024,2048]{1,0:T(8,128)}), f32[1024,512]{1,0:T(8,128)}) %reduce-scatter.2.cloned.1.call-update) | async-done | bytes 2097168 | tf_op jit(solution)/shard_map/reduce_scatter | solution.py:33
  154.7 6.4 %divide_bitcast_fusion = (f32[1,1024,512]{2,1,0:T(8,128)}, f32[1,1024,512]{2,1,0:T(8,128)}, f32[1,1024,512]{2,1,0:T(8,128)}) fusion(f32[1024,512]{1,0:T(8,128)} %reduce-scatter.2.cloned.1.call-done, f32[1,1024,512]{2,1,0:T(8,128)} %param.10, f32[1,1024,512]{2,1,0:T(8,128)} %param.11), kind=kLoop, calls=%fused_computation.6 | loop fusion | flops 6291456 | bytes 12582912 | tf_op jit(solution)/shard_map/stack | solution.py:38
Async XLA Ops:
  7.2 52.0 %copy-start = (bf16[1,1024,1024]{2,1,0:T(8,128)(2,1)S(1)}, bf16[1,1024,1024]{2,1,0:T(8,128)(2,1)}, u32[]{:S(2)}) copy-start(bf16[1,1024,1024]{2,1,0:T(8,128)(2,1)} %param.6) | copy-start | bytes 6291460
  7.2 52.0 %all-gather.3.cloned.1.call-start = ((), (), s32[]{:S(2)}) async-start(), calls=%async_computation.2 | async-start | bytes 4718592 | tf_op jit(solution)/shard_map/all_gather | solution.py:32
  7.9 146.8 %reduce-scatter.2.cloned.1.call-start = ((), (), s32[]{:S(2)}) async-start(), calls=%async_computation.1 | async-start | bytes 10485760 | tf_op jit(solution)/shard_map/reduce_scatter | solution.py:33
Sparse Core Ops, SparseCore 0:
  9.6 49.5 all-gather.2
  68.3 86.3 reduce-scatter.1
where the time goes:
time: 168 us
  waiting for transfers between devices  94.6 us (56%)
  blocking collectives  40.4 us (24%)
  between operations  14 us (8%)
  other arithmetic  9.91 us (6%)
  matrix products  8.95 us (5%)
    all_gather x1, waiting for transfers between devices, shards(): lax.all_gather(grad_rows, 'tp', axis=0, tiled=True)  51.2 us
    reduce_scatter x1, waiting for transfers between devices, shards(): lax.psum_scatter(local_grad, 'dp', scatter_dimension=1, tiled=True)  42.7 us
    psum x1, blocking collectives, shards(): gain_grad = lax.psum(local_terms, ('dp', 'tp')) / replicas  40.4 us
    dot_general x1, matrix products, row_adder(): lax.dot_general(inputs, arrived, (((0,), (0,)), ((), ())), preferred_elem...  8.95 us
    another operation x1, other arithmetic, shards(): jnp.stack(updates)  6.44 us
  transfers between devices with their start and end apart: 2, of which 2 were waited for; matrix products, arithmetic and copies ran while one was open for 2% of the time, Pallas kernels for 0%

commit v1 on v0

v1 whole, which is shorter than its diff:
```python
import functools

import jax
import jax.numpy as jnp
from jax import lax
from jax.experimental import pallas as pl
from jax.experimental.pallas import tpu as pltpu
from jax.sharding import PartitionSpec as P

beta_one = 0.9
beta_two = 0.95
correct_one = 0.19
correct_two = 0.0975
epsilon = 1e-08
PIECES = 4


def adam_update(mean_grad, first_old, second_old):
    new_first = beta_one * first_old + (1.0 - beta_one) * mean_grad
    new_second = beta_two * second_old + (1.0 - beta_two) * mean_grad * mean_grad
    update = new_first / correct_one / (jnp.sqrt(new_second / correct_two) + epsilon)
    return (new_first, new_second, update)


def kernel(
    n_dp, n_tp, x_hbm, g_hbm, a_hbm, b_hbm, sum_ref, gain_ref,
    xs, kv, a_buf, b_buf, gain_tp, gain_dp,
    local_sem, x_send, x_recv, a2a_send, a2a_recv,
    up_send, up_recv, down_send, down_recv, pair_send, pair_recv,
    gt_send, gt_recv, gd_send, gd_recv,
):
    dp = lax.axis_index("dp")
    tp = lax.axis_index("tp")
    z = tp // 2
    core = tp % 2
    n_z = n_tp // 2
    rows = g_hbm.shape[0]
    cols = kv.shape[2]
    tokens = x_hbm.shape[0]
    piece = tokens // PIECES

    def dp_peer(o):
        return jnp.bitwise_xor(dp, o)

    def tp_peer(o):
        return lax.rem(tp + o, n_tp)

    locals_ = [
        pltpu.make_async_copy(a_hbm, a_buf, local_sem.at[0]),
        pltpu.make_async_copy(b_hbm, b_buf, local_sem.at[1]),
        pltpu.make_async_copy(
            g_hbm.at[:, pl.ds(pl.multiple_of(dp * cols, cols), cols)],
            kv.at[dp, pl.ds(pl.multiple_of(tp * rows, rows), rows), :],
            local_sem.at[2],
        ),
        pltpu.make_async_copy(x_hbm, xs.at[dp], local_sem.at[3]),
    ]
    for copy in locals_:
        copy.start()

    barrier = pltpu.get_barrier_semaphore()
    for o in range(1, n_dp):
        pl.semaphore_signal(barrier, inc=1, device_id={"dp": dp_peer(o)}, device_id_type=pl.DeviceIdType.MESH)
    for o in range(1, n_tp):
        pl.semaphore_signal(barrier, inc=1, device_id={"tp": tp_peer(o)}, device_id_type=pl.DeviceIdType.MESH)
    pl.semaphore_wait(barrier, n_dp - 1 + n_tp - 1)

    sent = []

    def remote(src, dst, send, recv, where):
        return pltpu.make_async_remote_copy(
            src_ref=src, dst_ref=dst, send_sem=send, recv_sem=recv,
            device_id=where, device_id_type=pl.DeviceIdType.MESH,
        )

    my_rows = pl.ds(pl.multiple_of(tp * rows, rows), rows)
    a2a = []
    for o in range(1, n_dp):
        peer = dp_peer(o)
        copy = remote(
            g_hbm.at[:, pl.ds(pl.multiple_of(peer * cols, cols), cols)],
            kv.at[dp, my_rows, :], a2a_send.at[o], a2a_recv.at[o], {"dp": peer},
        )
        copy.start()
        a2a.append(copy)
        sent.append(copy)

    def x_copy(src, origin, c, o_recv, o_to, send):
        part = pl.ds(c * piece, piece)
        return remote(
            src.at[part, :], xs.at[origin, part, :], send, x_recv.at[o_recv, c],
            {"dp": dp_peer(o_to)},
        )

    square = n_dp == 4
    orders = {o: list(range(PIECES)) for o in range(1, n_dp)}
    half = PIECES // 2
    if square:
        orders[2] = list(range(half, PIECES)) + list(range(half))
        orders[3] = []

    def send_own(i):
        for o in range(1, n_dp):
            if i < len(orders[o]):
                c = orders[o][i]
                copy = x_copy(x_hbm, dp, c, o, o, x_send.at[o, c])
                copy.start()
                sent.append(copy)

    def got(o, c):
        x_copy(xs.at[dp_peer(o)], dp_peer(o), c, o, o, x_send.at[o, c]).wait_recv()

    def forward(i):
        for o, o_to in ((1, 2), (2, 1)):
            c = orders[o][i]
            got(o, c)
            copy = x_copy(xs.at[dp_peer(o)], dp_peer(o), c, 3, o_to, x_send.at[3, c])
            copy.start()
            sent.append(copy)

    send_own(0)
    send_own(1)

    locals_[0].wait()
    locals_[1].wait()
    wide = gain_tp.shape[2]
    lines = gain_tp.shape[1]
    for j in range(lines):
        s = pl.ds(j * wide, wide)
        products = a_buf[:, s].astype(jnp.float32) * b_buf[:, s].astype(jnp.float32)
        gain_tp[tp, pl.ds(j, 1), :] = jnp.sum(products, axis=0, keepdims=True)
    tp_copies = []
    for o in range(1, n_tp):
        copy = remote(gain_tp.at[tp], gain_tp.at[tp], gt_send.at[o], gt_recv.at[o], {"tp": tp_peer(o)})
        copy.start()
        sent.append(copy)
        tp_copies.append(copy)

    def block(b, c):
        return kv.at[:, pl.ds(pl.multiple_of((2 * b + c) * rows, rows), rows), :]

    other = 2 * z + 1 - core

    def to_pair(b):
        return remote(block(b, core), block(b, core), pair_send.at[b], pair_recv.at[b], {"tp": other})

    def up(s):
        b = z - s + 1
        return remote(block(b, core), block(b, core), up_send.at[s], up_recv.at[s], {"tp": tp + 2})

    def down(s):
        b = z + s - 1
        return remote(block(b, core), block(b, core), down_send.at[s], down_recv.at[s], {"tp": tp - 2})

    def up_got(s):
        b = z - s
        return remote(block(b, core), block(b, core), up_send.at[s], up_recv.at[s], {"tp": other})

    def down_got(s):
        b = z + s
        return remote(block(b, core), block(b, core), down_send.at[s], down_recv.at[s], {"tp": other})

    locals_[2].wait()
    for o in range(1, n_dp):
        a2a[o - 1].wait_recv()

    for s in range(1, n_z + 1):
        if s > 1:
            @pl.when(z - s + 1 >= 0)
            def _():
                up_got(s - 1).wait_recv()

        if s < n_z:
            @pl.when((z - s + 1 >= 0) & (z + 1 < n_z))
            def _():
                up(s).start()

        if s > 1:
            @pl.when(z + s - 1 < n_z)
            def _():
                down_got(s - 1).wait_recv()

        if s < n_z:
            @pl.when((z + s - 1 < n_z) & (z - 1 >= 0))
            def _():
                down(s).start()

        if s == 1:
            to_pair(z).start()
        else:
            @pl.when(z - s + 1 >= 0)
            def _():
                to_pair(z - s + 1).start()

            @pl.when(z + s - 1 < n_z)
            def _():
                to_pair(z + s - 1).start()

        if s == 1:
            for copy in tp_copies:
                copy.wait_recv()
            gain_dp[dp, :, :] = jnp.sum(gain_tp[...], axis=0)
            for o in range(1, n_dp):
                copy = remote(gain_dp.at[dp], gain_dp.at[dp], gd_send.at[o], gd_recv.at[o], {"dp": dp_peer(o)})
                copy.start()
                sent.append(copy)
            for i in range(2, PIECES):
                send_own(i)
        if square and 2 <= s < 2 + half:
            forward(s - 2)
    if square:
        for i in range(max(n_z - 1, 0), half):
            forward(i)

    for b in range(n_z):
        remote(block(b, 1 - core), block(b, 1 - core), pair_send.at[b], pair_recv.at[b], {"tp": other}).wait_recv()

    width = min(256, sum_ref.shape[0])

    def multiply(origin, start, size, first=False):
        @pl.loop(0, sum_ref.shape[0] // width)
        def _(f):
            at = pl.ds(pl.multiple_of(f * width, width), width)
            part = lax.dot_general(
                xs[origin, pl.ds(start, size), at], kv[origin, pl.ds(start, size), :],
                (((0,), (0,)), ((), ())), preferred_element_type=jnp.float32,
            )
            if first:
                sum_ref[at, :] = part
            else:
                sum_ref[at, :] += part

    locals_[3].wait()
    multiply(dp, 0, tokens, True)
    for o in range(1, n_dp):
        if square and o == 3:
            continue
        for c in orders[o]:
            if not (square and c in orders[o][:half]):
                got(o, c)
        multiply(dp_peer(o), 0, tokens)

    for o in range(1, n_dp):
        remote(gain_dp.at[dp_peer(o)], gain_dp.at[dp_peer(o)], gd_send.at[o], gd_recv.at[o], {"dp": dp_peer(o)}).wait_recv()
    gain_ref[...] = jnp.sum(gain_dp[...], axis=0) / n_dp

    if square:
        for i in range(half):
            for o in (1, 2):
                c = orders[o][i]
                got(3, c)
                multiply(dp_peer(3), c * piece, piece)

    for copy in sent:
        copy.wait_send()
    for s in range(1, n_z):
        @pl.when((z - s + 1 >= 0) & (z + 1 < n_z))
        def _():
            up(s).wait_send()

        @pl.when((z + s - 1 < n_z) & (z - 1 >= 0))
        def _():
            down(s).wait_send()
    for b in range(n_z):
        to_pair(b).wait_send()


def shards(n_dp, n_tp, proj_in, kv_grad, normed, norm_grad, first_moment, second_moment):
    layers, tokens, features = proj_in.shape
    rows, width = kv_grad.shape[1:]
    model = normed.shape[2]
    cols = width // n_dp
    lines = 8
    dma = pltpu.SemaphoreType.DMA
    n_z = n_tp // 2
    firsts, seconds, updates, gains = [], [], [], []
    for layer in range(layers):
        total, gain = pl.pallas_call(
            functools.partial(kernel, n_dp, n_tp),
            out_shape=(
                jax.ShapeDtypeStruct((features, cols), jnp.float32),
                jax.ShapeDtypeStruct((lines, model // lines), jnp.float32),
            ),
            in_specs=[pl.BlockSpec(memory_space=pl.ANY)] * 4,
            out_specs=(pl.BlockSpec(memory_space=pltpu.VMEM), pl.BlockSpec(memory_space=pltpu.VMEM)),
            scratch_shapes=[
                pltpu.VMEM((n_dp, tokens, features), jnp.bfloat16),
                pltpu.VMEM((n_dp, n_tp * rows, cols), jnp.bfloat16),
                pltpu.VMEM((rows, model), jnp.bfloat16),
                pltpu.VMEM((rows, model), jnp.bfloat16),
                pltpu.VMEM((n_tp, lines, model // lines), jnp.float32),
                pltpu.VMEM((n_dp, lines, model // lines), jnp.float32),
                dma((4,)),
                dma((n_dp, PIECES)), dma((n_dp, PIECES)),
                dma((n_dp,)), dma((n_dp,)),
                dma((n_z,)), dma((n_z,)), dma((n_z,)), dma((n_z,)),
                dma((n_z,)), dma((n_z,)),
                dma((n_tp,)), dma((n_tp,)), dma((n_dp,)), dma((n_dp,)),
            ],
            compiler_params=pltpu.CompilerParams(
                collective_id=layer, has_side_effects=True, vmem_limit_bytes=60 * 1024 * 1024,
            ),
        )(proj_in[layer], kv_grad[layer], normed[layer], norm_grad[layer])
        new_first, new_second, update = adam_update(total / n_dp, first_moment[layer], second_moment[layer])
        firsts.append(new_first)
        seconds.append(new_second)
        updates.append(update)
        gains.append(gain.reshape(model))
    return (jnp.stack(firsts), jnp.stack(seconds), jnp.stack(updates), jnp.stack(gains))


def solution(mesh):
    return jax.shard_map(
        functools.partial(shards, mesh.shape["dp"], mesh.shape["tp"]),
        mesh=mesh,
        in_specs=(
            P(None, "dp", "tp"),
            P(None, ("dp", "tp"), None),
            P(None, ("dp", "tp"), None),
            P(None, ("dp", "tp"), None),
            P(None, "tp", "dp"),
            P(None, "tp", "dp"),
        ),
        out_specs=(P(None, "tp", "dp"), P(None, "tp", "dp"), P(None, "tp", "dp"), P()),
        check_vma=False,
    )
```

time: 168 us -> 94.7 us (0.56)
  waiting for transfers between devices: 94.6 us -> 0 us
  Pallas kernels: 0 us -> 86.6 us
  blocking collectives: 40.4 us -> 0 us
  between operations: 14 us -> 0.65 us
  matrix products: 8.95 us -> 0 us
  other arithmetic: 9.91 us -> 5.81 us
    pallas_call x0 -> x1, Pallas kernels: none -> 86.6 us  [shards(): pl.pallas_call(functools.partial(kernel, n_dp, n_tp), out_shape=(jax.Shap...]
    all_gather x1 -> x0, waiting for transfers between devices: 51.2 us -> none  [shards(): lax.all_gather(grad_rows, 'tp', axis=0, tiled=True)]
    reduce_scatter x1 -> x0, waiting for transfers between devices: 42.7 us -> none  [shards(): lax.psum_scatter(local_grad, 'dp', scatter_dimension=1, tiled=True)]
    psum x1 -> x0, blocking collectives: 40.4 us -> none  [shards(): gain_grad = lax.psum(local_terms, ('dp', 'tp')) / replicas]
    dot_general x1 -> x0, matrix products: 8.95 us -> none  [row_adder(): lax.dot_general(inputs, arrived, (((0,), (0,)), ((), ())), preferred_elem...]
    reduce_sum x1 -> x0, other arithmetic: 2.83 us -> none  [shards(): jnp.sum(norm_grad.astype(jnp.float32) * normed.astype(jnp.float32), axis=1)]
  transfers between devices with their start and end apart: 2 -> 0, of which waited for: 2 -> 0; matrix products, arithmetic and copies ran while one was open for 2% -> 0% of each run, Pallas kernels for 0% -> 0%
where the time goes in v1:
time: 94.7 us; the launch traced here: 94.5 us
  Pallas kernels  86.6 us (91%)
  other arithmetic  5.81 us (6%)
  local copies, waits for them, and re-layouts  1.41 us (1%)
    pallas_call x1, Pallas kernels, shards(): pl.pallas_call(functools.partial(kernel, n_dp, n_tp), out_shape=(jax.Shap...  86.6 us
    another operation x1, other arithmetic, shards(): jnp.stack(updates)  5.81 us

profile of v1, /device:TPU:0, one launch (start us, length us, event | category | flops | bytes accessed | tf_op | source)
XLA Modules:
  0.0 94.5 jit_solution(4602089025900275508)
XLA Ops:
  0.6 0.0 copy-start
  0.6 86.6 %shard_map.93 = (f32[1024,512]{1,0:T(8,128)}, f32[8,1024]{1,0:T(8,128)}) custom-call(bf16[1024,1024]{1,0:T(8,128)(2,1)} %bitcast.25, bf16[128,2048]{1,0:T(8,128)(2,1)} %bitcast.28, bf16[128,8192]{1,0:T(8,128)(2,1)} %bitcast.26, bf16[128,8192]{1,0:T(8,128)(2,1)} %bitcast.27), custom_call_target="tpu_custom_call" | custom-call | tf_op jit(solution)/shard_map/pallas_call | solution.py:278
  87.3 1.4 %copy.10 = f32[1,1,8,1024]{3,1,2,0:T(1,128)} copy(f32[1,1,8,1024]{3,2,1,0:T(8,128)} %bitcast.30) | data formatting | bytes 65536
  88.7 0.0 copy-done
  88.7 5.8 %divide_bitcast_fusion = (f32[1,1024,512]{2,1,0:T(8,128)}, f32[1,1024,512]{2,1,0:T(8,128)}, f32[1,1024,512]{2,1,0:T(8,128)}) fusion(f32[1024,512]{1,0:T(8,128)} %get-tuple-element.6, f32[1,1024,512]{2,1,0:T(8,128)S(1)} %copy-done, f32[1,1024,512]{2,1,0:T(8,128)} %param.11), kind=kLoop, calls=%fused_computation.2 | loop fusion | flops 6291456 | bytes 12582912 | tf_op jit(solution)/shard_map/stack | solution.py:309
Async XLA Ops:
  0.6 88.0 %copy-start = (f32[1,1024,512]{2,1,0:T(8,128)S(1)}, f32[1,1024,512]{2,1,0:T(8,128)}, u32[]{:S(2)}) copy-start(f32[1,1024,512]{2,1,0:T(8,128)} %param.10) | copy-start | bytes 6291460

commit v2 on v1

--- a/solution.py
+++ b/solution.py
@@ -13,6 +13,7 @@
 correct_two = 0.0975
 epsilon = 1e-08
 PIECES = 4
+HEADS = 6
 
 
 def adam_update(mean_grad, first_old, second_old):
@@ -265,6 +266,322 @@
         to_pair(b).wait_send()
 
 
+def square_kernel(
+    n_tp, x_hbm, g_hbm, a_hbm, b_hbm, sum_ref, gain_ref,
+    xs, xb, kv, kvp, part, arrived, a_buf, b_buf, gain_pair, gain_z, gain_dp,
+    local_sem, head_send, head_recv, whole_send, whole_recv, fwd_send, fwd_recv,
+    part_send, part_recv, a2a_send, a2a_recv,
+    up_send, up_recv, down_send, down_recv, pair_send, pair_recv,
+    gp_send, gp_recv, gz_send, gz_recv, gd_send, gd_recv,
+):
+    n_dp = 4
+    dp = lax.axis_index("dp")
+    tp = lax.axis_index("tp")
+    z = tp // 2
+    core = tp % 2
+    n_z = n_tp // 2
+    rows = g_hbm.shape[0]
+    cols = kv.shape[2]
+    tokens, features = x_hbm.shape
+    head = part.shape[0]
+    tail = features - head
+    chunk = head // HEADS
+    half = tokens // 2
+    other = 2 * z + 1 - core
+    sent = []
+
+    def dp_peer(o):
+        return jnp.bitwise_xor(dp, o)
+
+    def remote(src, dst, send, recv, where):
+        return pltpu.make_async_remote_copy(
+            src_ref=src, dst_ref=dst, send_sem=send, recv_sem=recv,
+            device_id=where, device_id_type=pl.DeviceIdType.MESH,
+        )
+
+    def go(copy):
+        copy.start()
+        sent.append(copy)
+
+    my_rows = pl.ds(pl.multiple_of(tp * rows, rows), rows)
+
+    def g_cols(d):
+        return g_hbm.at[:, pl.ds(pl.multiple_of(d * cols, cols), cols)]
+
+    locals_ = [
+        pltpu.make_async_copy(g_cols(dp_peer(2)), kvp.at[0, my_rows, :], local_sem.at[0]),
+        pltpu.make_async_copy(a_hbm, a_buf, local_sem.at[1]),
+        pltpu.make_async_copy(b_hbm, b_buf, local_sem.at[2]),
+        pltpu.make_async_copy(g_cols(dp), kv.at[dp, my_rows, :], local_sem.at[3]),
+        pltpu.make_async_copy(x_hbm, xs.at[0], local_sem.at[4]),
+    ]
+    for copy in locals_:
+        copy.start()
+
+    barrier = pltpu.get_barrier_semaphore()
+    for o in range(1, n_dp):
+        pl.semaphore_signal(barrier, inc=1, device_id={"dp": dp_peer(o)}, device_id_type=pl.DeviceIdType.MESH)
+    for o in range(1, n_tp):
+        pl.semaphore_signal(barrier, inc=1, device_id={"tp": lax.rem(tp + o, n_tp)}, device_id_type=pl.DeviceIdType.MESH)
+    pl.semaphore_wait(barrier, n_dp - 1 + n_tp - 1)
+
+    pair_base = dp // 2 * 2
+    groups = [
+        kvp.at[pl.ds(0, 1)],
+        kvp.at[pl.ds(1, 1)],
+        kv.at[pl.ds(pair_base, 2)],
+        kv.at[pl.ds(2 - pair_base, 2)],
+    ]
+
+    def block(g, b, c):
+        return groups[g].at[:, pl.ds(pl.multiple_of((2 * b + c) * rows, rows), rows), :]
+
+    def to_pair(g, b):
+        return remote(block(g, b, core), block(g, b, core), pair_send.at[g, b], pair_recv.at[g, b], {"tp": other})
+
+    def from_pair(g, b):
+        return remote(block(g, b, 1 - core), block(g, b, 1 - core), pair_send.at[g, b], pair_recv.at[g, b], {"tp": other})
+
+    def up(g, s):
+        b = z - s + 1
+        return remote(block(g, b, core), block(g, b, core), up_send.at[g, s], up_recv.at[g, s], {"tp": tp + 2})
+
+    def down(g, s):
+        b = z + s - 1
+        return remote(block(g, b, core), block(g, b, core), down_send.at[g, s], down_recv.at[g, s], {"tp": tp - 2})
+
+    def up_got(g, s):
+        b = z - s
+        return remote(block(g, b, core), block(g, b, core), up_send.at[g, s], up_recv.at[g, s], {"tp": other})
+
+    def down_got(g, s):
+        b = z + s
+        return remote(block(g, b, core), block(g, b, core), down_send.at[g, s], down_recv.at[g, s], {"tp": other})
+
+    def chain(g, s):
+        if s > 1:
+            @pl.when(z - s + 1 >= 0)
+            def _():
+                up_got(g, s - 1).wait_recv()
+
+        if s < n_z:
+            @pl.when((z - s + 1 >= 0) & (z + 1 < n_z))
+            def _():
+                up(g, s).start()
+
+        if s > 1:
+            @pl.when(z + s - 1 < n_z)
+            def _():
+                down_got(g, s - 1).wait_recv()
+
+        if s < n_z:
+            @pl.when((z + s - 1 < n_z) & (z - 1 >= 0))
+            def _():
+                down(g, s).start()
+
+        if s == 1:
+            to_pair(g, z).start()
+        else:
+            @pl.when(z - s + 1 >= 0)
+            def _():
+                to_pair(g, z - s + 1).start()
+
+            @pl.when(z + s - 1 < n_z)
+            def _():
+                to_pair(g, z + s - 1).start()
+
+    def complete(g):
+        for b in range(n_z):
+            from_pair(g, b).wait_recv()
+
+    swap = remote(g_cols(dp_peer(3)), kvp.at[1, my_rows, :], a2a_send.at[0], a2a_recv.at[0], {"dp": dp_peer(1)})
+    go(swap)
+    locals_[0].wait()
+    chain(0, 1)
+
+    def a2a(o, origin):
+        return remote(g_cols(dp_peer(o)), kv.at[origin, my_rows, :], a2a_send.at[o], a2a_recv.at[o], {"dp": dp_peer(o)})
+
+    for o in range(1, n_dp):
+        go(a2a(o, dp))
+
+    tail_at = pl.ds(head, tail)
+
+    def head_copy(k):
+        at = pl.ds(k * chunk, chunk)
+        return remote(x_hbm.at[:, at], xs.at[1, :, at], head_send.at[k], head_recv.at[k], {"dp": dp_peer(1)})
+
+    def tail_copy(o, h):
+        at = pl.ds(h * half, half)
+        dst = xs.at[1, at, tail_at] if o == 1 else xb.at[0, at, :]
+        return remote(x_hbm.at[at, tail_at], dst, whole_send.at[o, h], whole_recv.at[o, h], {"dp": dp_peer(o)})
+
+    def forward(h):
+        at = pl.ds(h * half, half)
+        src = xs.at[1, at, tail_at] if h == 0 else xb.at[0, at, :]
+        return remote(src, xb.at[1, at, :], fwd_send.at[h], fwd_recv.at[h], {"dp": dp_peer(2 - h)})
+
+    early = HEADS // 2
+    for k in range(early):
+        go(head_copy(k))
+    go(tail_copy(2, 1))
+    go(tail_copy(2, 0))
+
+    locals_[1].wait()
+    locals_[2].wait()
+    wide = gain_pair.shape[2]
+
+    def gain_lines(lo, hi):
+        for j in range(lo, hi):
+            at = pl.ds(j * wide, wide)
+            products = a_buf[:, at].astype(jnp.float32) * b_buf[:, at].astype(jnp.float32)
+            gain_pair[core, pl.ds(j, 1), :] = jnp.sum(products, axis=0, keepdims=True)
+
+    lines = gain_pair.shape[1]
+    gain_lines(0, lines)
+    swap.wait_recv()
+    chain(1, 1)
+    gain_core = remote(gain_pair.at[core], gain_pair.at[core], gp_send.at[0], gp_recv.at[0], {"tp": other})
+    go(gain_core)
+    for s in range(2, n_z + 1):
+        chain(0, s)
+        chain(1, s)
+
+    gain_core.wait_recv()
+    gain_z[z, :, :] = jnp.sum(gain_pair[...], axis=0)
+    for o in range(1, n_z):
+        go(remote(gain_z.at[z], gain_z.at[z], gz_send.at[o], gz_recv.at[o], {"tp": lax.rem(tp + 2 * o, n_tp)}))
+
+    for o in (1, 2, 3):
+        a2a(o, dp_peer(o)).wait_recv()
+    locals_[3].wait()
+    chain(2, 1)
+    locals_[4].wait()
+    for k in range(early, HEADS):
+        go(head_copy(k))
+    complete(0)
+    complete(1)
+
+    def dot(x, w):
+        return lax.dot_general(x, w, (((0,), (0,)), ((), ())), preferred_element_type=jnp.float32)
+
+    def part_copy(k):
+        at = pl.ds(k * chunk, chunk)
+        return remote(part.at[at, :], arrived.at[at, :], part_send.at[k], part_recv.at[k], {"dp": dp_peer(2)})
+
+    for k in range(HEADS):
+        at = pl.ds(k * chunk, chunk)
+        head_copy(k).wait_recv()
+        part[at, :] = dot(xs[0, :, at], kvp[0]) + dot(xs[1, :, at], kvp[1])
+        go(part_copy(k))
+        if k == 1:
+            for o in range(1, n_z):
+                copy = remote(
+                    gain_z.at[lax.rem(z + o, n_z)], gain_z.at[lax.rem(z + o, n_z)],
+                    gz_send.at[n_z - o], gz_recv.at[n_z - o], {"tp": other},
+                )
+                copy.wait_recv()
+            gain_dp[dp, :, :] = jnp.sum(gain_z[...], axis=0)
+            for o in range(1, n_dp):
+                go(remote(gain_dp.at[dp], gain_dp.at[dp], gd_send.at[o], gd_recv.at[o], {"dp": dp_peer(o)}))
+            chain(2, 2)
+        if k == 2:
+            go(tail_copy(1, 0))
+            go(tail_copy(1, 1))
+        if k == 3:
+            tail_copy(2, 1).wait_recv()
+            go(forward(1))
+            chain(2, 3)
+            chain(3, 1)
+        if k == HEADS - 2:
+            for s in range(4, n_z + 1):
+                chain(2, s)
+    complete(2)
+    chain(3, 2)
+
+    def head_sum(k):
+        at = pl.ds(k * chunk, chunk)
+        sum_ref[at, :] = dot(xs[0, :, at], kv[dp]) + dot(xs[1, :, at], kv[dp_peer(1)])
+
+    for k in range(HEADS // 2):
+        head_sum(k)
+    tail_copy(1, 0).wait_recv()
+    go(forward(0))
+    chain(3, 3)
+    for k in range(HEADS // 2, HEADS):
+        head_sum(k)
+    tail_copy(1, 1).wait_recv()
+    sum_ref[tail_at, :] = dot(xs[0, :, tail_at], kv[dp]) + dot(xs[1, :, tail_at], kv[dp_peer(1)])
+    for s in range(4, n_z + 1):
+        chain(3, s)
+    for o in range(1, n_dp):
+        remote(gain_dp.at[dp_peer(o)], gain_dp.at[dp_peer(o)], gd_send.at[o], gd_recv.at[o], {"dp": dp_peer(o)}).wait_recv()
+    gain_ref[...] = jnp.sum(gain_dp[...], axis=0) / n_dp
+    for k in range(HEADS):
+        at = pl.ds(k * chunk, chunk)
+        part_copy(k).wait_recv()
+        sum_ref[at, :] += arrived[at, :]
+    complete(3)
+    tail_copy(2, 0).wait_recv()
+    sum_ref[tail_at, :] += dot(xb[0], kv[dp_peer(2)])
+    for h in (1, 0):
+        forward(h).wait_recv()
+        at = pl.ds(h * half, half)
+        sum_ref[tail_at, :] += dot(xb[1, at, :], kv[dp_peer(3), at, :])
+
+    for copy in sent:
+        copy.wait_send()
+    for g in range(len(groups)):
+        for s in range(1, n_z):
+            @pl.when((z - s + 1 >= 0) & (z + 1 < n_z))
+            def _():
+                up(g, s).wait_send()
+
+            @pl.when((z + s - 1 < n_z) & (z - 1 >= 0))
+            def _():
+                down(g, s).wait_send()
+        for b in range(n_z):
+            to_pair(g, b).wait_send()
+
+
+def square_call(layer, n_tp, x, g, a, b):
+    tokens, features = x.shape
+    rows, width = g.shape
+    model = a.shape[1]
+    n_dp = 4
+    cols = width // n_dp
+    lines = 8
+    n_z = n_tp // 2
+    head = features // (HEADS + 2) * HEADS
+    dma = pltpu.SemaphoreType.DMA
+    bf16, f32 = jnp.bfloat16, jnp.float32
+    buffers = [
+        ((2, tokens, features), bf16), ((2, tokens, features - head), bf16),
+        ((n_dp, tokens, cols), bf16), ((2, tokens, cols), bf16),
+        ((head, cols), f32), ((head, cols), f32),
+        ((rows, model), bf16), ((rows, model), bf16),
+        ((2, lines, model // lines), f32), ((n_z, lines, model // lines), f32), ((n_dp, lines, model // lines), f32),
+    ]
+    return pl.pallas_call(
+        functools.partial(square_kernel, n_tp),
+        out_shape=(
+            jax.ShapeDtypeStruct((features, cols), f32),
+            jax.ShapeDtypeStruct((lines, model // lines), f32),
+        ),
+        in_specs=[pl.BlockSpec(memory_space=pl.ANY)] * 4,
+        out_specs=(pl.BlockSpec(memory_space=pltpu.VMEM), pl.BlockSpec(memory_space=pltpu.VMEM)),
+        scratch_shapes=[pltpu.VMEM(shape, dtype) for shape, dtype in buffers] + [
+            dma((5,)), dma((HEADS,)), dma((HEADS,)), dma((3, 2)), dma((3, 2)), dma((2,)), dma((2,)),
+            dma((HEADS,)), dma((HEADS,)), dma((n_dp,)), dma((n_dp,)),
+        ] + [dma((4, n_z))] * 6 + [
+            dma((1,)), dma((1,)), dma((n_z,)), dma((n_z,)), dma((n_dp,)), dma((n_dp,)),
+        ],
+        compiler_params=pltpu.CompilerParams(
+            collective_id=layer, has_side_effects=True, vmem_limit_bytes=60 * 1024 * 1024,
+        ),
+    )(x, g, a, b)
+
+
 def shards(n_dp, n_tp, proj_in, kv_grad, normed, norm_grad, first_moment, second_moment):
     layers, tokens, features = proj_in.shape
     rows, width = kv_grad.shape[1:]
@@ -275,32 +592,35 @@
     n_z = n_tp // 2
     firsts, seconds, updates, gains = [], [], [], []
     for layer in range(layers):
-        total, gain = pl.pallas_call(
-            functools.partial(kernel, n_dp, n_tp),
-            out_shape=(
-                jax.ShapeDtypeStruct((features, cols), jnp.float32),
-                jax.ShapeDtypeStruct((lines, model // lines), jnp.float32),
-            ),
-            in_specs=[pl.BlockSpec(memory_space=pl.ANY)] * 4,
-            out_specs=(pl.BlockSpec(memory_space=pltpu.VMEM), pl.BlockSpec(memory_space=pltpu.VMEM)),
-            scratch_shapes=[
-                pltpu.VMEM((n_dp, tokens, features), jnp.bfloat16),
-                pltpu.VMEM((n_dp, n_tp * rows, cols), jnp.bfloat16),
-                pltpu.VMEM((rows, model), jnp.bfloat16),
-                pltpu.VMEM((rows, model), jnp.bfloat16),
-                pltpu.VMEM((n_tp, lines, model // lines), jnp.float32),
-                pltpu.VMEM((n_dp, lines, model // lines), jnp.float32),
-                dma((4,)),
-                dma((n_dp, PIECES)), dma((n_dp, PIECES)),
-                dma((n_dp,)), dma((n_dp,)),
-                dma((n_z,)), dma((n_z,)), dma((n_z,)), dma((n_z,)),
-                dma((n_z,)), dma((n_z,)),
-                dma((n_tp,)), dma((n_tp,)), dma((n_dp,)), dma((n_dp,)),
-            ],
-            compiler_params=pltpu.CompilerParams(
-                collective_id=layer, has_side_effects=True, vmem_limit_bytes=60 * 1024 * 1024,
-            ),
-        )(proj_in[layer], kv_grad[layer], normed[layer], norm_grad[layer])
+        if n_dp == 4 and features % (128 * (HEADS + 2)) == 0 and n_tp >= 6:
+            total, gain = square_call(layer, n_tp, proj_in[layer], kv_grad[layer], normed[layer], norm_grad[layer])
+        else:
+            total, gain = pl.pallas_call(
+                functools.partial(kernel, n_dp, n_tp),
+                out_shape=(
+                    jax.ShapeDtypeStruct((features, cols), jnp.float32),
+                    jax.ShapeDtypeStruct((lines, model // lines), jnp.float32),
+                ),
+                in_specs=[pl.BlockSpec(memory_space=pl.ANY)] * 4,
+                out_specs=(pl.BlockSpec(memory_space=pltpu.VMEM), pl.BlockSpec(memory_space=pltpu.VMEM)),
+                scratch_shapes=[
+                    pltpu.VMEM((n_dp, tokens, features), jnp.bfloat16),
+                    pltpu.VMEM((n_dp, n_tp * rows, cols), jnp.bfloat16),
+                    pltpu.VMEM((rows, model), jnp.bfloat16),
+                    pltpu.VMEM((rows, model), jnp.bfloat16),
+                    pltpu.VMEM((n_tp, lines, model // lines), jnp.float32),
+                    pltpu.VMEM((n_dp, lines, model // lines), jnp.float32),
+                    dma((4,)),
+                    dma((n_dp, PIECES)), dma((n_dp, PIECES)),
+                    dma((n_dp,)), dma((n_dp,)),
+                    dma((n_z,)), dma((n_z,)), dma((n_z,)), dma((n_z,)),
+                    dma((n_z,)), dma((n_z,)),
+                    dma((n_tp,)), dma((n_tp,)), dma((n_dp,)), dma((n_dp,)),
+                ],
+                compiler_params=pltpu.CompilerParams(
+                    collective_id=layer, has_side_effects=True, vmem_limit_bytes=60 * 1024 * 1024,
+                ),
+            )(proj_in[layer], kv_grad[layer], normed[layer], norm_grad[layer])
         new_first, new_second, update = adam_update(total / n_dp, first_moment[layer], second_moment[layer])
         firsts.append(new_first)
         seconds.append(new_second)

time: 94.7 us -> 83.5 us (0.88)
  Pallas kernels: 86.6 us -> 75.4 us
    pallas_call x1, Pallas kernels: 86.6 us -> 75.4 us  [square_call(): pl.pallas_call(functools.partial(square_kernel, n_tp), out_shape=(jax.Sha...]
where the time goes in v2:
time: 83.5 us; the launch traced here: 83.3 us
  Pallas kernels  75.4 us (90%)
  other arithmetic  5.81 us (7%)
  local copies, waits for them, and re-layouts  1.41 us (2%)
    pallas_call x1, Pallas kernels, square_call(): pl.pallas_call(functools.partial(square_kernel, n_tp), out_shape=(jax.Sha...  75.4 us
    another operation x1, other arithmetic, shards(): jnp.stack(updates)  5.81 us

profile of v2, /device:TPU:0, one launch (start us, length us, event | category | flops | bytes accessed | tf_op | source)
XLA Modules:
  0.0 83.3 jit_solution(3068307730649528311)
XLA Ops:
  0.6 0.0 copy-start
  0.6 75.4 %shard_map.93 = (f32[1024,512]{1,0:T(8,128)}, f32[8,1024]{1,0:T(8,128)}) custom-call(bf16[1024,1024]{1,0:T(8,128)(2,1)} %bitcast.25, bf16[128,2048]{1,0:T(8,128)(2,1)} %bitcast.28, bf16[128,8192]{1,0:T(8,128)(2,1)} %bitcast.26, bf16[128,8192]{1,0:T(8,128)(2,1)} %bitcast.27), custom_call_target="tpu_custom_call" | custom-call | tf_op jit(solution)/shard_map/pallas_call | solution.py:565
  76.0 1.4 %copy.10 = f32[1,1,8,1024]{3,1,2,0:T(1,128)} copy(f32[1,1,8,1024]{3,2,1,0:T(8,128)} %bitcast.30) | data formatting | bytes 65536
  77.5 0.0 copy-done
  77.5 5.8 %divide_bitcast_fusion = (f32[1,1024,512]{2,1,0:T(8,128)}, f32[1,1024,512]{2,1,0:T(8,128)}, f32[1,1024,512]{2,1,0:T(8,128)}) fusion(f32[1024,512]{1,0:T(8,128)} %get-tuple-element.6, f32[1,1024,512]{2,1,0:T(8,128)S(1)} %copy-done, f32[1,1024,512]{2,1,0:T(8,128)} %param.11), kind=kLoop, calls=%fused_computation.2 | loop fusion | flops 6291456 | bytes 12582912 | tf_op jit(solution)/shard_map/stack | solution.py:629
Async XLA Ops:
  0.6 76.8 %copy-start = (f32[1,1024,512]{2,1,0:T(8,128)S(1)}, f32[1,1024,512]{2,1,0:T(8,128)}, u32[]{:S(2)}) copy-start(f32[1,1024,512]{2,1,0:T(8,128)} %param.10) | copy-start | bytes 6291460

commit v3 on v2

--- a/solution.py
+++ b/solution.py
@@ -516,7 +516,9 @@
         chain(3, s)
     for o in range(1, n_dp):
         remote(gain_dp.at[dp_peer(o)], gain_dp.at[dp_peer(o)], gd_send.at[o], gd_recv.at[o], {"dp": dp_peer(o)}).wait_recv()
-    gain_ref[...] = jnp.sum(gain_dp[...], axis=0) / n_dp
+    total_gain = jnp.sum(gain_dp[...], axis=0) / n_dp
+    for i in range(wide // 128):
+        gain_ref[pl.ds(i, lines, stride=wide // 128), :] = total_gain[:, i * 128:(i + 1) * 128]
     for k in range(HEADS):
         at = pl.ds(k * chunk, chunk)
         part_copy(k).wait_recv()
@@ -566,9 +568,9 @@
         functools.partial(square_kernel, n_tp),
         out_shape=(
             jax.ShapeDtypeStruct((features, cols), f32),
-            jax.ShapeDtypeStruct((lines, model // lines), f32),
+            jax.ShapeDtypeStruct((model // 128, 128), f32),
         ),
-        in_specs=[pl.BlockSpec(memory_space=pl.ANY)] * 4,
+        in_specs=[pl.BlockSpec(memory_space=pltpu.HBM)] * 4,
         out_specs=(pl.BlockSpec(memory_space=pltpu.VMEM), pl.BlockSpec(memory_space=pltpu.VMEM)),
         scratch_shapes=[pltpu.VMEM(shape, dtype) for shape, dtype in buffers] + [
             dma((5,)), dma((HEADS,)), dma((HEADS,)), dma((3, 2)), dma((3, 2)), dma((2,)), dma((2,)),
@@ -577,7 +579,7 @@
             dma((1,)), dma((1,)), dma((n_z,)), dma((n_z,)), dma((n_dp,)), dma((n_dp,)),
         ],
         compiler_params=pltpu.CompilerParams(
-            collective_id=layer, has_side_effects=True, vmem_limit_bytes=60 * 1024 * 1024,
+            collective_id=layer, has_side_effects=True, vmem_limit_bytes=50 * 1024 * 1024,
         ),
     )(x, g, a, b)
 
@@ -601,7 +603,7 @@
                     jax.ShapeDtypeStruct((features, cols), jnp.float32),
                     jax.ShapeDtypeStruct((lines, model // lines), jnp.float32),
                 ),
-                in_specs=[pl.BlockSpec(memory_space=pl.ANY)] * 4,
+                in_specs=[pl.BlockSpec(memory_space=pltpu.HBM)] * 4,
                 out_specs=(pl.BlockSpec(memory_space=pltpu.VMEM), pl.BlockSpec(memory_space=pltpu.VMEM)),
                 scratch_shapes=[
                     pltpu.VMEM((n_dp, tokens, features), jnp.bfloat16),

time: 83.5 us -> 79.9 us (0.957)
  other arithmetic: 5.81 us -> 3.59 us
  Pallas kernels: 75.4 us -> 73.8 us
    another operation x1, other arithmetic: 5.81 us -> 3.59 us  [shards(): jnp.stack(updates)]
    pallas_call x1, Pallas kernels: 75.4 us -> 73.8 us  [square_call(): pl.pallas_call(functools.partial(square_kernel, n_tp), out_shape=(jax.Sha...]
where the time goes in v3:
time: 79.9 us; the launch traced here: 79.8 us
  Pallas kernels  73.8 us (92%)
  other arithmetic  3.59 us (4%)
  local copies, waits for them, and re-layouts  1.66 us (2%)
    pallas_call x1, Pallas kernels, square_call(): pl.pallas_call(functools.partial(square_kernel, n_tp), out_shape=(jax.Sha...  73.8 us
    another operation x1, other arithmetic, shards(): jnp.stack(updates)  3.59 us
    unnamed x7, local copies, waits for them, and re-layouts  1.66 us

profile of v3, /device:TPU:0, one launch (start us, length us, event | category | flops | bytes accessed | tf_op | source)
XLA Modules:
  0.0 79.8 jit_solution(6663524581731930500)
XLA Ops:
  0.6 0.0 copy-start
  0.6 1.0 %copy-done = bf16[1,128,2048]{2,1,0:T(8,128)(2,1)S(1)} copy-done((bf16[1,128,2048]{2,1,0:T(8,128)(2,1)S(1)}, bf16[1,128,2048]{2,1,0:T(8,128)(2,1)}, u32[]{:S(2)}) %copy-start) | copy-done | bytes 524312
  1.7 0.0 copy-start.1
  1.7 0.0 copy-start.2
  1.7 73.8 %shard_map.93 = (f32[1024,512]{1,0:T(8,128)S(1)}, f32[64,128]{1,0:T(8,128)S(1)}) custom-call(bf16[1024,1024]{1,0:T(8,128)(2,1)} %bitcast.25, bf16[128,2048]{1,0:T(8,128)(2,1)S(1)} %bitcast.23, bf16[128,8192]{1,0:T(8,128)(2,1)} %bitcast.26, bf16[128,8192]{1,0:T(8,128)(2,1)} %bitcast.27), custom_call_target="tpu_custom_call" | custom-call | tf_op jit(solution)/shard_map/pallas_call | solution.py:567
  75.5 0.0 copy-done.1
  75.5 0.0 copy-done.2
  75.6 3.6 %divide_bitcast_fusion = (f32[1,1024,512]{2,1,0:T(8,128)}, f32[1,1024,512]{2,1,0:T(8,128)}, f32[1,1024,512]{2,1,0:T(8,128)}) fusion(f32[1024,512]{1,0:T(8,128)S(1)} %get-tuple-element.6, f32[1,1024,512]{2,1,0:T(8,128)S(1)} %copy-done.1, f32[1,1024,512]{2,1,0:T(8,128)S(1)} %copy-done.2), kind=kLoop, calls=%fused_computation.2 | loop fusion | flops 6291456 | bytes 12582912 | tf_op jit(solution)/shard_map/stack | solution.py:631
  79.1 0.6 copy.11
Async XLA Ops:
  0.6 1.0 %copy-start = (bf16[1,128,2048]{2,1,0:T(8,128)(2,1)S(1)}, bf16[1,128,2048]{2,1,0:T(8,128)(2,1)}, u32[]{:S(2)}) copy-start(bf16[1,128,2048]{2,1,0:T(8,128)(2,1)} %param.7) | copy-start | bytes 1572868
  1.7 73.9 %copy-start.1 = (f32[1,1024,512]{2,1,0:T(8,128)S(1)}, f32[1,1024,512]{2,1,0:T(8,128)}, u32[]{:S(2)}) copy-start(f32[1,1024,512]{2,1,0:T(8,128)} %param.10) | copy-start | bytes 6291460
  1.7 73.9 %copy-start.2 = (f32[1,1024,512]{2,1,0:T(8,128)S(1)}, f32[1,1024,512]{2,1,0:T(8,128)}, u32[]{:S(2)}) copy-start(f32[1,1024,512]{2,1,0:T(8,128)} %param.11) | copy-start | bytes 6291460
